TPU v7x, 32 devices: a whole 2x2x4 slice. The times are simulated.
32 devices in a mesh: dp: 2 (over x), tp: 16 (over y, z, core).
Axes of the slice: x: 2, y: 2, z: 4, core: 2. Of those that a mesh axis runs over, the one named last changes fastest.
Arguments:
- x: bfloat16 [7168, 5120], P(('dp', 'tp')), parts along dimension 0
- w_gate: bfloat16 [5120, 32768], P(None, 'tp')
- w_up: bfloat16 [5120, 32768], P(None, 'tp')
- w_down: bfloat16 [32768, 5120], P('tp')
Outputs:
- output: bfloat16 [7168, 5120], P(('dp', 'tp')), parts along dimension 0
There are 2 independent parts. A program takes and returns all parts, laid end to end along the dimension named above; an argument that names none is the same for every part.
All inputs are finite; a program needn't handle non-finite values.
Results may differ from a plain program's by a relative error of at most 0.016.
Values are sent between devices in bfloat16 or wider.
A program may use at most 2 GiB of HBM per device.

v0:
```python
import jax
import jax.numpy as jnp
from jax import lax
from jax.sharding import PartitionSpec as P


def solution(mesh):
    def step(x, w_gate, w_up, w_down):
        rows = lax.all_gather(x, "tp", axis=0, tiled=True)
        gate = jnp.dot(rows, w_gate, preferred_element_type=jnp.float32)
        up = jnp.dot(rows, w_up, preferred_element_type=jnp.float32)
        hidden = (jax.nn.silu(gate) * up).astype(jnp.bfloat16)
        term = jnp.dot(hidden, w_down, preferred_element_type=jnp.float32).astype(jnp.bfloat16)
        return lax.psum_scatter(term, "tp", scatter_dimension=0, tiled=True)

    return jax.shard_map(
        step,
        mesh=mesh,
        in_specs=(P(("dp", "tp"), None), P(None, "tp"), P(None, "tp"), P("tp", None)),
        out_specs=P(("dp", "tp"), None),
        check_vma=False,
    )
```

profile of v0, /device:TPU:0, one launch (start us, length us, event | category | flops | bytes accessed | tf_op | source)
XLA Modules:
  0.0 813.9 jit_solution(1872742499329247959)
XLA Ops:
  6.5 0.0 all-gather.2.cloned.1.call-start
  6.5 0.7 all-gather.2.cloned.1.call-update
  7.3 0.0 reduce-scatter.2.cloned.1.call-start
  7.3 187.2 %all-gather.2.cloned.1.call-done = bf16[3584,5120]{1,0:T(8,128)(2,1)} async-done(((bf16[224,5120]{1,0:T(8,128)(2,1)}), bf16[3584,5120]{1,0:T(8,128)(2,1)}) %all-gather.2.cloned.1.call-update) | async-done | bytes 36700176 | tf_op jit(solution)/shard_map/all_gather | solution.py:9
  194.5 85.4 %fusion = f32[3584,2048]{1,0:T(8,128)} fusion(bf16[3584,5120]{1,0:T(8,128)(2,1)} %all-gather.2.cloned.1.call-done, bf16[5120,2048]{1,0:T(8,128)(2,1)} %param.5), kind=kOutput, calls=%fused_computation.2 | convolution fusion | flops 75161927680 | bytes 87031808 | tf_op jit(solution)/shard_map/dot_general | solution.py:10
  279.9 87.7 %multiply_convert_fusion = bf16[3584,2048]{1,0:T(8,128)(2,1)} fusion(f32[3584,2048]{1,0:T(8,128)} %fusion, bf16[3584,5120]{1,0:T(8,128)(2,1)} %all-gather.2.cloned.1.call-done, bf16[5120,2048]{1,0:T(8,128)(2,1)} %param.6), kind=kOutput, calls=%fused_computation.1 | convolution fusion | flops 75205967872 | bytes 101711872 | tf_op jit(solution)/shard_map/dot_general | solution.py:11
  367.6 85.7 %convolution_convert_fusion = bf16[3584,5120]{1,0:T(8,128)(2,1)} fusion(bf16[3584,2048]{1,0:T(8,128)(2,1)} %multiply_convert_fusion, bf16[2048,5120]{1,0:T(8,128)(2,1)} %param.7), kind=kOutput, calls=%fused_computation | convolution fusion | flops 75180277760 | bytes 72351744 | tf_op jit(solution)/shard_map/dot_general | solution.py:13
  453.3 0.0 reduce-scatter.2.cloned.1.call-update
  453.3 353.8 %reduce-scatter.2.cloned.1.call-done = bf16[224,5120]{1,0:T(8,128)(2,1)} async-done(((bf16[3584,5120]{1,0:T(8,128)(2,1)}), bf16[224,5120]{1,0:T(8,128)(2,1)}) %reduce-scatter.2.cloned.1.call-update) | async-done | bytes 2293776 | tf_op jit(solution)/shard_map/reduce_scatter | solution.py:14
Async XLA Ops:
  6.5 187.9 %all-gather.2.cloned.1.call-start = ((), (), s32[]{:S(2)}) async-start(), calls=%async_computation.1 | async-start | bytes 38993920 | tf_op jit(solution)/shard_map/all_gather | solution.py:9
  7.3 799.8 %reduce-scatter.2.cloned.1.call-start = ((), (), s32[]{:S(2)}) async-start(), calls=%async_computation.2 | async-start | bytes 38993920 | tf_op jit(solution)/shard_map/reduce_scatter | solution.py:14
Sparse Core Ops, SparseCore 0:
  8.9 185.4 all-gather.1
  453.4 353.5 reduce-scatter.1
where the time goes:
time: 814 us
  waiting for transfers between devices  542 us (67%)
  matrix products  259 us (32%)
  between operations  13.4 us (2%)
    reduce_scatter x1, waiting for transfers between devices, step(): return lax.psum_scatter(term, 'tp', scatter_dimension=0, tiled=True)  354 us
    all_gather x1, waiting for transfers between devices, step(): rows = lax.all_gather(x, 'tp', axis=0, tiled=True)  187 us
    dot_general x1, matrix products, step(): up = jnp.dot(rows, w_up, preferred_element_type=jnp.float32)  87.7 us
    dot_general x1, matrix products, step(): jnp.dot(hidden, w_down, preferred_element_type=jnp.float32)  85.7 us
    dot_general x1, matrix products, step(): gate = jnp.dot(rows, w_gate, preferred_element_type=jnp.float32)  85.4 us
  transfers between devices with their start and end apart: 2, of which 2 were waited for; matrix products, arithmetic and copies ran while one was open for 0% of the time, Pallas kernels for 0%

commit v1 on v0

v1 whole, which is shorter than its diff:
```python
import jax
import jax.numpy as jnp
from jax import lax
from jax.experimental import pallas as pl
from jax.experimental.pallas import tpu as pltpu
from jax.sharding import PartitionSpec as P

MESH = pl.DeviceIdType.MESH
TILE = 512


def _device(r, c):
    y = r // 4
    z = r + y * (7 - 2 * r)
    return (y * 4 + z) * 2 + c


def _mlp_kernel(
    x, wg_hbm, wu_hbm, wd_hbm,
    out, xg, hid, parts, sums,
    wg, wu, xbuf, wd, hbuf, term, other, pin, rin,
    ag_send, ag_recv, dd_send, dd_recv, rs_send, rs_recv, pt_send, pt_recv,
    w_sem, x_sem, h_sem, hl_sem, wd_sem, in_sem, y_sem,
):
    half = x.shape[0] // 2
    d, ff = wg.shape
    ftiles = ff // TILE
    dtiles = d // TILE
    t = lax.axis_index("tp")
    c = t % 2
    z = (t // 2) % 4
    y = t // 8
    r = z + y * (7 - 2 * z)
    right = _device((r + 1) % 8, c)
    left = _device((r + 7) % 8, c)
    partner = t + 1 - 2 * c
    ring = (right, left)

    def rows(j, h, rel, n=1):
        return pl.ds(pl.multiple_of(((j * 2 + h) * 2 + rel) * half, half), n * half)

    def remote(src, dst, s, q, i, dev):
        return pltpu.make_async_remote_copy(
            src_ref=src, dst_ref=dst, send_sem=s.at[i], recv_sem=q.at[i],
            device_id={"tp": dev}, device_id_type=MESH,
        )

    def gathered(i, way):
        if way == 0:
            return (i + 1) // 2, (i + 1) % 2
        return (8 - (i + 1) // 2) % 8, 1 - (i + 1) % 2

    def ag_copy(m, way, own=False):
        h = m % 2 if way == 0 else 1 - m % 2
        j, jn = gathered(m + 1, way)[0], None
        src_j = m // 2 if way == 0 else (8 - m // 2) % 8
        src = x.at[pl.ds(h * half, half)] if own else xg.at[rows(src_j, h, 0)]
        return remote(src, xg.at[rows(j, h, 0)], ag_send, ag_recv, way * 7 + m, ring[way])

    def dd_copy(i, way, own=False):
        j, h = gathered(i, way)
        src = x.at[pl.ds(h * half, half)] if own else xg.at[rows(j, h, 0)]
        return remote(src, xg.at[rows(j, h, 1)], dd_send, dd_recv, way * 8 + i, partner)

    def w_copy(k, n):
        cols = pl.ds(pl.multiple_of(n * TILE, TILE), TILE)
        return pltpu.make_async_copy(
            (wg_hbm, wu_hbm)[k].at[:, cols], (wg, wu)[k].at[:, cols], w_sem.at[k, n]
        )

    def x_load(i, way):
        j, h = gathered(i, way)
        return pltpu.make_async_copy(
            xg.at[rows(j, h, 0, 2)], xbuf.at[pl.ds(way * 2 * half, 2 * half)], x_sem.at[way]
        )

    def h_store(i, way):
        j, h = gathered(i, way)
        return pltpu.make_async_copy(hbuf.at[way], hid.at[rows(j, h, 0, 2)], h_sem.at[way])

    barrier = pltpu.get_barrier_semaphore()
    for dev in (right, left, partner):
        pl.semaphore_signal(barrier, inc=1, device_id={"tp": dev}, device_id_type=MESH)
    pl.semaphore_wait(barrier, 3)

    for m in range(2):
        for way in range(2):
            ag_copy(m, way, own=True).start()
    for way in range(2):
        dd_copy(0, way, own=True).start()
    bounce = pltpu.make_async_copy(x, xbuf.at[pl.ds(2 * half, 2 * half)], x_sem.at[0])
    bounce.start()
    for n in range(ftiles):
        for k in range(2):
            w_copy(k, n).start()
    bounce.wait()
    for h in range(2):
        pltpu.make_async_copy(
            xbuf.at[pl.ds((2 + h) * half, half)], xg.at[rows(0, h, 0)], x_sem.at[h]
        ).start()
    for h in range(2):
        pltpu.make_async_copy(
            xbuf.at[pl.ds((2 + h) * half, half)], xg.at[rows(0, h, 0)], x_sem.at[h]
        ).wait()
    for way in range(2):
        dd_copy(0, way, own=True).wait_recv()
    x_load(0, 0).start()

    def stage(i, _):
        def tile(way, n):
            @pl.when((i == 0) & (way == 0))
            def _():
                for k in range(2):
                    w_copy(k, n).wait()

            cols = pl.ds(pl.multiple_of(n * TILE, TILE), TILE)
            block = xbuf[pl.ds(pl.multiple_of(way * 2 * half, 2 * half), 2 * half), :]
            gate = jnp.dot(block, wg[:, cols], preferred_element_type=jnp.float32)
            up = jnp.dot(block, wu[:, cols], preferred_element_type=jnp.float32)
            hbuf[way, :, cols] = (jax.nn.silu(gate) * up).astype(jnp.bfloat16)

        def work(s, _):
            way, n = s // ftiles, s % ftiles

            @pl.when(s == 0)
            def _():
                x_load(i, 0).wait()
                x_load(i, 1).start()

                @pl.when(i > 0)
                def _():
                    h_store(i - 1, 0).wait()

            @pl.when(s == ftiles)
            def _():
                h_store(i, 0).start()
                x_load(i, 1).wait()

                @pl.when(i > 0)
                def _():
                    h_store(i - 1, 1).wait()

            @pl.when((s == 2 * ftiles - 1) & (i < 7))
            def _():
                for w in range(2):
                    ag_copy(i, w).wait_recv()

                    @pl.when(i < 5)
                    def _():
                        ag_copy(i + 2, w).start()

                    dd_copy(i + 1, w).start()

            tile(way, n)
            return 0

        lax.fori_loop(0, 2 * ftiles, work, 0)
        h_store(i, 1).start()

        @pl.when(i < 7)
        def _():
            for w in range(2):
                dd_copy(i + 1, w).wait_recv()
            x_load(i + 1, 0).start()

        return 0

    lax.fori_loop(0, 8, stage, 0)
    for way in range(2):
        h_store(7, way).wait()

    def drain(m, _):
        for way in range(2):
            ag_copy(m, way).wait_send()
        return 0

    lax.fori_loop(0, 7, drain, 0)

    def drain_pair(i, _):
        for way in range(2):
            dd_copy(i, way).wait_send()
        return 0

    lax.fori_loop(0, 8, drain_pair, 0)

    def target(q):
        m, way = q // 2, q % 2
        sign = 1 - 2 * way
        j = (12 + sign * ((m + 1) // 2)) % 8
        h = way + sign * (m % 2)
        return j, h

    def h_load(q):
        j, h = target(q)
        return pltpu.make_async_copy(hid.at[rows(j, h, 0, 2)], hbuf.at[q % 2], hl_sem.at[q % 2])

    def wd_copy(g):
        n = g % dtiles
        cols = pl.ds(pl.multiple_of(n * TILE, TILE), TILE)
        return pltpu.make_async_copy(wd_hbm.at[:, cols], wd.at[g % 2], wd_sem.at[g % 2])

    def slot(ref, i):
        return ref.at[pl.ds(pl.multiple_of(i * half, half), half)]

    def pt_copy(q):
        return remote(other.at[q % 2], slot(parts, q), pt_send, pt_recv, q, partner)

    def rs_copy(m, way):
        i = way * 7 + m
        return remote(slot(xbuf, way * 2 + m % 2), slot(sums, i), rs_send, rs_recv, i, ring[way])

    h_load(0).start()
    wd_copy(0).start()

    def down(q):
        h_load(q).wait()

        @pl.when(q < 15)
        def _():
            h_load(q + 1).start()

        @pl.when(q >= 2)
        def _():
            pt_copy(q - 2).wait_send()

        def tile(n, _):
            g = q * dtiles + n
            wd_copy(g).wait()

            @pl.when(g + 1 < 16 * dtiles)
            def _():
                wd_copy(g + 1).start()

            cols = pl.ds(pl.multiple_of(n * TILE, TILE), TILE)
            prod = jnp.dot(hbuf[q % 2], wd[g % 2], preferred_element_type=jnp.float32)
            term[q % 2, :, cols] = prod[:half]
            other[q % 2, :, cols] = prod[half:].astype(jnp.bfloat16)
            return 0

        lax.fori_loop(0, dtiles, tile, 0)
        pt_copy(q).start()

    def fetch(src, dst, i):
        return pltpu.make_async_copy(src, dst, in_sem.at[i])

    def add(q, to, sources):
        def tile(n, _):
            cols = pl.ds(pl.multiple_of(n * TILE, TILE), TILE)
            total = term[q % 2, :, cols] + pin[:, cols].astype(jnp.float32)
            for s in range(sources):
                total += rin[s, :, cols].astype(jnp.float32)
            to[:, cols] = total.astype(jnp.bfloat16)
            return 0

        lax.fori_loop(0, dtiles, tile, 0)

    def send(q, way):
        m = q // 2
        pt_copy(q).wait_recv()
        own = fetch(slot(parts, q), pin, 0)
        own.start()

        @pl.when(m >= 2)
        def _():
            rs_copy(m - 2, way).wait_recv()
            got = fetch(slot(sums, way * 7 + m - 2), rin.at[0], 1)
            got.start()
            rs_copy(m - 2, way).wait_send()
            got.wait()

        own.wait()
        to = slot(xbuf, way * 2 + m % 2)

        @pl.when(m >= 2)
        def _():
            add(q, to, 1)

        @pl.when(m < 2)
        def _():
            add(q, to, 0)

        rs_copy(m, way).start()

    def finish(q):
        way = q - 14
        h = 1 - way
        pt_copy(q).wait_recv()
        own = fetch(slot(parts, q), pin, 0)
        own.start()
        last = ((5, 6), (6, 5))[way]
        for w in range(2):
            rs_copy(last[w], w).wait_recv()
            fetch(slot(sums, w * 7 + last[w]), rin.at[w], 1 + w).start()
        for w in range(2):
            fetch(slot(sums, w * 7 + last[w]), rin.at[w], 1 + w).wait()
        own.wait()
        add(q, other.at[way], 2)
        pltpu.make_async_copy(other.at[way], out.at[pl.ds(h * half, half)], y_sem.at[way]).start()

    down(0)

    def step(q, _):
        @pl.when(q < 16)
        def _():
            down(q)

        for way in range(2):
            @pl.when((q - 1) % 2 == way)
            def _():
                send(q - 1, way)
        return 0

    lax.fori_loop(1, 15, step, 0)
    down(15)
    pt_copy(14).wait_send()
    finish(14)
    pt_copy(15).wait_send()
    finish(15)
    for way in range(2):
        pltpu.make_async_copy(
            other.at[way], out.at[pl.ds((1 - way) * half, half)], y_sem.at[way]
        ).wait()
        for m in (5, 6):
            rs_copy(m, way).wait_send()


def solution(mesh):
    def step(x, w_gate, w_up, w_down):
        n, d = x.shape
        ff = w_gate.shape[1]
        half = n // 2
        bf = jnp.bfloat16
        hbm = pl.BlockSpec(memory_space=pl.ANY)
        dma = pltpu.SemaphoreType.DMA
        result = pl.pallas_call(
            _mlp_kernel,
            out_shape=[
                jax.ShapeDtypeStruct((n, d), bf),
                jax.ShapeDtypeStruct((16 * n, d), bf),
                jax.ShapeDtypeStruct((16 * n, ff), bf),
                jax.ShapeDtypeStruct((16 * half, d), bf),
                jax.ShapeDtypeStruct((14 * half, d), bf),
            ],
            in_specs=[hbm] * 4,
            out_specs=[hbm] * 5,
            scratch_shapes=[
                pltpu.VMEM((d, ff), bf),
                pltpu.VMEM((d, ff), bf),
                pltpu.VMEM((4 * half, d), bf),
                pltpu.VMEM((2, ff, TILE), bf),
                pltpu.VMEM((2, n, ff), bf),
                pltpu.VMEM((2, half, d), jnp.float32),
                pltpu.VMEM((2, half, d), bf),
                pltpu.VMEM((half, d), bf),
                pltpu.VMEM((2, half, d), bf),
                dma((14,)), dma((14,)), dma((16,)), dma((16,)),
                dma((14,)), dma((14,)), dma((16,)), dma((16,)),
                dma((2, ff // TILE)), dma((2,)), dma((2,)), dma((2,)), dma((2,)), dma((3,)), dma((2,)),
            ],
            compiler_params=pltpu.CompilerParams(
                collective_id=0, has_side_effects=True, vmem_limit_bytes=67043328
            ),
        )(x, w_gate, w_up, w_down)
        return result[0]

    return jax.shard_map(
        step,
        mesh=mesh,
        in_specs=(P(("dp", "tp"), None), P(None, "tp"), P(None, "tp"), P("tp", None)),
        out_specs=P(("dp", "tp"), None),
        check_vma=False,
    )
```

time: 814 us -> 511 us (0.63)
  waiting for transfers between devices: 542 us -> 0 us
  Pallas kernels: 0 us -> 502 us
  matrix products: 259 us -> 0 us
  between operations: 13.4 us -> 0.01 us
    pallas_call x0 -> x1, Pallas kernels: none -> 502 us  [step(): pl.pallas_call(_mlp_kernel, out_shape=[jax.ShapeDtypeStruct((n, d), bf),...]
    reduce_scatter x1 -> x0, waiting for transfers between devices: 354 us -> none  [step(): return lax.psum_scatter(term, 'tp', scatter_dimension=0, tiled=True)]
    dot_general x3 -> x0, matrix products: 259 us -> none  [the longest x1 87.7 us: step(): up = jnp.dot(rows, w_up, preferred_element_type=jnp.float32)]
    all_gather x1 -> x0, waiting for transfers between devices: 187 us -> none  [step(): rows = lax.all_gather(x, 'tp', axis=0, tiled=True)]
  transfers between devices with their start and end apart: 2 -> 0, of which waited for: 2 -> 0; matrix products, arithmetic and copies ran while one was open for 0% -> 0% of each run, Pallas kernels for 0% -> 0%
where the time goes in v1:
time: 511 us; the launch traced here: 505 us
  Pallas kernels  502 us (98%)
    pallas_call x1, Pallas kernels, step(): pl.pallas_call(_mlp_kernel, out_shape=[jax.ShapeDtypeStruct((n, d), bf),...  502 us

profile of v1, /device:TPU:0, one launch (start us, length us, event | category | flops | bytes accessed | tf_op | source)
XLA Modules:
  0.0 505.2 jit_solution(1520933887446606393)
XLA Ops:
  0.0 502.0 %shard_map.46 = (bf16[224,5120]{1,0:T(8,128)(2,1)}, bf16[3584,5120]{1,0:T(8,128)(2,1)}, bf16[3584,2048]{1,0:T(8,128)(2,1)}, bf16[1792,5120]{1,0:T(8,128)(2,1)}, bf16[1568,5120]{1,0:T(8,128)(2,1)}) custom-call(bf16[224,5120]{1,0:T(8,128)(2,1)} %x.1, bf16[5120,2048]{1,0:T(8,128)(2,1)} %wg_hbm.1, bf16[5120,2048]{1,0:T(8,128)(2,1)} %wu_hbm.1, ...), custom_call_target="tpu_custom_call" | custom-call | tf_op jit(solution)/shard_map/pallas_call | solution.py:335
  502.0 3.2 copy.6

commit v2 on v1

v2 whole, which is shorter than its diff:
```python
import jax
import jax.numpy as jnp
from jax import lax
from jax.experimental import pallas as pl
from jax.experimental.pallas import tpu as pltpu
from jax.sharding import PartitionSpec as P

MESH = pl.DeviceIdType.MESH
TILE = 512
EARLY = 256


def _device(r, c):
    y = r // 4
    z = r + y * (7 - 2 * r)
    return (y * 4 + z) * 2 + c


def _mlp_kernel(
    x, wg_hbm, wu_hbm, wd_hbm,
    out, xg, hid, parts, sums,
    w, xbuf, wd, hbuf, term, other, pin, rin,
    ag_send, ag_recv, dd_send, dd_recv, rs_send, rs_recv, pt_send, pt_recv,
    w_sem, x_sem, h_sem, wd_sem, early_sem, in_sem, y_sem,
):
    half = x.shape[0] // 2
    n_rows = 2 * half
    d, ff = wg_hbm.shape
    ftiles = ff // TILE
    dtiles = d // TILE
    wide = ff // 2
    t = lax.axis_index("tp")
    c = t % 2
    z = (t // 2) % 4
    y = t // 8
    r = z + y * (7 - 2 * z)
    right = _device((r + 1) % 8, c)
    left = _device((r + 7) % 8, c)
    partner = t + 1 - 2 * c
    ring = (right, left)

    def span(i, n, size):
        return pl.ds(pl.multiple_of(i * size, size), n * size)

    def rows(j, h, rel, n=1):
        return span((j * 2 + h) * 2 + rel, n, half)

    def remote(src, dst, s, q, i, dev):
        return pltpu.make_async_remote_copy(
            src_ref=src, dst_ref=dst, send_sem=s.at[i], recv_sem=q.at[i],
            device_id={"tp": dev}, device_id_type=MESH,
        )

    def gathered(i, way):
        if way == 0:
            return (i + 1) // 2, (i + 1) % 2
        return (8 - (i + 1) // 2) % 8, 1 - (i + 1) % 2

    def ag_copy(m, way, own=False):
        h = m % 2 if way == 0 else 1 - m % 2
        j = gathered(m + 1, way)[0]
        src_j = m // 2 if way == 0 else (8 - m // 2) % 8
        src = x.at[pl.ds(h * half, half)] if own else xg.at[rows(src_j, h, 0)]
        return remote(src, xg.at[rows(j, h, 0)], ag_send, ag_recv, way * 7 + m, ring[way])

    def dd_copy(i, way, own=False):
        j, h = gathered(i, way)
        src = x.at[pl.ds(h * half, half)] if own else xg.at[rows(j, h, 0)]
        return remote(src, xg.at[rows(j, h, 1)], dd_send, dd_recv, way * 8 + i, partner)

    def w_copy(k, n):
        cols = span(n, 1, TILE)
        return pltpu.make_async_copy(
            (wg_hbm, wu_hbm)[k].at[:, cols], w.at[pl.ds(k * d, d), cols], w_sem.at[k, n]
        )

    def x_load(i, way):
        j, h = gathered(i, way)
        return pltpu.make_async_copy(
            xg.at[rows(j, h, 0, 2)], xbuf.at[pl.ds(way * n_rows, n_rows)], x_sem.at[way]
        )

    def h_store(i, way):
        j, h = gathered(i, way)
        return pltpu.make_async_copy(
            hbuf.at[pl.ds(way * n_rows, n_rows)], hid.at[rows(j, h, 0, 2)], h_sem.at[way]
        )

    def slot(ref, i):
        return ref.at[span(i, 1, half)]

    def pt_copy(q):
        return remote(other.at[q % 2], slot(parts, q), pt_send, pt_recv, q, partner)

    def rs_copy(m, way, first=False):
        i = way * 7 + m
        src = rin.at[way] if first else slot(xbuf, way * 2 + m % 2)
        return remote(src, slot(sums, i), rs_send, rs_recv, i, ring[way])

    def fetch(src, dst, i):
        return pltpu.make_async_copy(src, dst, in_sem.at[i])

    def add(q, to, sources):
        def tile(n, _):
            cols = span(n, 1, TILE)
            total = term[q % 2, :, cols] + pin[:, cols].astype(jnp.float32)
            for s in range(sources):
                total += rin[s, :, cols].astype(jnp.float32)
            to[:, cols] = total.astype(jnp.bfloat16)
            return 0

        lax.fori_loop(0, dtiles, tile, 0)

    def early_copy(n):
        return pltpu.make_async_copy(
            wd_hbm.at[:, span(n, 1, EARLY)], wd.at[n % 4], early_sem.at[n % 4]
        )

    def early_terms():
        def tile(n, _):
            early_copy(n).wait()

            @pl.when(n + 3 < d // EARLY)
            def _():
                early_copy(n + 3).start()

            cols = span(n, 1, EARLY)
            prod = jnp.dot(hbuf[...], wd[n % 4], preferred_element_type=jnp.float32)
            term[1, :, cols] = prod[:half]
            other[1, :, cols] = prod[half:n_rows].astype(jnp.bfloat16)
            term[0, :, cols] = prod[n_rows : n_rows + half]
            other[0, :, cols] = prod[n_rows + half :].astype(jnp.bfloat16)
            return 0

        lax.fori_loop(0, d // EARLY, tile, 0)
        for q in range(2):
            pt_copy(q).start()

    def early_send():
        for q in range(2):
            pt_copy(q).wait_recv()
            own = fetch(slot(parts, q), pin, 0)
            own.start()
            own.wait()
            add(q, rin.at[q], 0)
            rs_copy(0, q, first=True).start()

    barrier = pltpu.get_barrier_semaphore()
    for dev in (right, left, partner):
        pl.semaphore_signal(barrier, inc=1, device_id={"tp": dev}, device_id_type=MESH)
    pl.semaphore_wait(barrier, 3)

    for m in range(2):
        for way in range(2):
            ag_copy(m, way, own=True).start()
    for way in range(2):
        dd_copy(0, way, own=True).start()
    bounce = pltpu.make_async_copy(x, xbuf.at[pl.ds(n_rows, n_rows)], x_sem.at[0])
    bounce.start()
    for n in range(ftiles):
        for k in range(2):
            w_copy(k, n).start()
    bounce.wait()
    stores = [
        pltpu.make_async_copy(
            xbuf.at[pl.ds((2 + h) * half, half)], xg.at[rows(0, h, 0)], x_sem.at[h]
        )
        for h in range(2)
    ]
    for s in stores:
        s.start()
    for s in stores:
        s.wait()
    for way in range(2):
        dd_copy(0, way, own=True).wait_recv()
    x_load(0, 0).start()

    def stage(i, _):
        @pl.when(i == 6)
        def _():
            early_terms()

        def work(s, _):
            way, n = (s // 2) % 2, s // 4 * 2 + s % 2

            for k in range(2):
                @pl.when(s == 2 * k)
                def _():
                    if k == 0:
                        x_load(i, 1).start()
                    x_load(i, k).wait()

                    @pl.when(i > 0)
                    def _():
                        h_store(i - 1, k).wait()

            @pl.when((s == 4) & (i == 6))
            def _():
                early_send()

            @pl.when((s == 4) & (i == 7))
            def _():
                for k in range(5):
                    wd_copy(k).start()

            @pl.when((s == 4) & (i == 5))
            def _():
                for k in range(3):
                    early_copy(k).start()

            @pl.when((s == 6) & (i < 7))
            def _():
                h_store(i, 0).start()

            @pl.when((s == 7) & (i < 7))
            def _():
                for k in range(2):
                    ag_copy(i, k).wait_recv()

                    @pl.when(i < 5)
                    def _():
                        ag_copy(i + 2, k).start()

                    dd_copy(i + 1, k).start()

            for k in range(2):
                @pl.when((i == 0) & (way == 0))
                def _():
                    w_copy(k, n).wait()

            cols = span(n, 1, TILE)
            block = xbuf[span(way, 1, n_rows), :]
            gate = jnp.dot(block, w[:d, cols], preferred_element_type=jnp.float32)
            up = jnp.dot(block, w[d:, cols], preferred_element_type=jnp.float32)
            hbuf[span(way, 1, n_rows), cols] = (jax.nn.silu(gate) * up).astype(jnp.bfloat16)
            return 0

        lax.fori_loop(0, 2 * ftiles, work, 0)

        @pl.when(i < 7)
        def _():
            h_store(i, 1).start()
            for k in range(2):
                dd_copy(i + 1, k).wait_recv()
            x_load(i + 1, 0).start()

        return 0

    def wd_copy(k):
        return pltpu.make_async_copy(
            wd_hbm.at[:, pl.ds(k * wide, wide)],
            w.at[pl.ds(k * ff, ff), pl.ds(0, wide)],
            wd_sem.at[k],
        )

    lax.fori_loop(0, 8, stage, 0)

    def target(q):
        m, way = q // 2, q % 2
        j = 4 + m // 2 + (1 - m % 2) - m // 6 + 2 * (m // 7)
        h = (1 - m % 2) * (1 - m // 6) + m // 7
        sign = 1 - 2 * way
        return (8 + sign * j) % 8, way + sign * h

    def h_load(q):
        j, h = target(q)
        return pltpu.make_async_copy(
            hid.at[rows(j, h, 0, 2)], hbuf.at[span(q % 2, 1, n_rows)], h_sem.at[q % 2]
        )

    def down(q):
        @pl.when(q >= 4)
        def _():
            h_load(q).wait()

        pt_copy(q - 2).wait_send()

        def tile(n, _):
            for k in range(5):
                @pl.when((q == 2) & (n == 2 * k))
                def _():
                    wd_copy(k).wait()

            block = w[span(n // 2, 1, ff), span(n % 2, 1, TILE)]
            prod = jnp.dot(
                hbuf[span(q % 2, 1, n_rows), :], block, preferred_element_type=jnp.float32
            )
            cols = span(n, 1, TILE)
            term[q % 2, :, cols] = prod[:half]
            other[q % 2, :, cols] = prod[half:].astype(jnp.bfloat16)
            return 0

        lax.fori_loop(0, dtiles, tile, 0)
        pt_copy(q).start()

        @pl.when(q < 14)
        def _():
            h_load(q + 2).start()

    def send(q, way):
        m = q // 2
        pt_copy(q).wait_recv()
        own = fetch(slot(parts, q), pin, 0)
        own.start()
        before = m - 2 + m // 6

        @pl.when(m >= 2)
        def _():
            rs_copy(before, way).wait_recv()
            rs_copy(m - 2, way).wait_send()
            got = fetch(slot(sums, way * 7 + before), rin.at[0], 1)
            got.start()
            got.wait()

        own.wait()
        to = slot(xbuf, way * 2 + m % 2)

        @pl.when(m >= 2)
        def _():
            add(q, to, 1)

        @pl.when(m < 2)
        def _():
            add(q, to, 0)

        rs_copy(m, way).start()

    def finish(q):
        way = q - 14
        h = 1 - way
        pt_copy(q).wait_recv()
        own = fetch(slot(parts, q), pin, 0)
        own.start()
        last = ((4, 6), (6, 4))[way]
        for k in range(2):
            rs_copy(last[k], k).wait_recv()
            fetch(slot(sums, k * 7 + last[k]), rin.at[k], 1 + k).start()
        for k in range(2):
            fetch(slot(sums, k * 7 + last[k]), rin.at[k], 1 + k).wait()
        own.wait()
        add(q, other.at[way], 2)
        pltpu.make_async_copy(other.at[way], out.at[pl.ds(h * half, half)], y_sem.at[way]).start()

    def step(q, _):
        down(q)
        for way in range(2):
            @pl.when((q > 2) & ((q - 1) % 2 == way))
            def _():
                send(q - 1, way)
        return 0

    lax.fori_loop(2, 15, step, 0)
    down(15)

    def drain(m, _):
        for way in range(2):
            ag_copy(m, way).wait_send()
        return 0

    def drain_pair(i, _):
        for way in range(2):
            dd_copy(i, way).wait_send()
        return 0

    lax.fori_loop(0, 7, drain, 0)
    lax.fori_loop(0, 8, drain_pair, 0)
    pt_copy(14).wait_send()
    finish(14)
    pt_copy(15).wait_send()
    finish(15)
    for way in range(2):
        pltpu.make_async_copy(
            other.at[way], out.at[pl.ds((1 - way) * half, half)], y_sem.at[way]
        ).wait()
        for m in (5, 6):
            rs_copy(m, way).wait_send()


def solution(mesh):
    def step(x, w_gate, w_up, w_down):
        n, d = x.shape
        ff = w_gate.shape[1]
        half = n // 2
        bf = jnp.bfloat16
        hbm = pl.BlockSpec(memory_space=pl.ANY)
        dma = pltpu.SemaphoreType.DMA
        result = pl.pallas_call(
            _mlp_kernel,
            out_shape=[
                jax.ShapeDtypeStruct((n, d), bf),
                jax.ShapeDtypeStruct((16 * n, d), bf),
                jax.ShapeDtypeStruct((16 * n, ff), bf),
                jax.ShapeDtypeStruct((16 * half, d), bf),
                jax.ShapeDtypeStruct((14 * half, d), bf),
            ],
            in_specs=[hbm] * 4,
            out_specs=[hbm] * 5,
            scratch_shapes=[
                pltpu.VMEM((2 * d, ff), bf),
                pltpu.VMEM((4 * half, d), bf),
                pltpu.VMEM((4, ff, EARLY), bf),
                pltpu.VMEM((2 * n, ff), bf),
                pltpu.VMEM((2, half, d), jnp.float32),
                pltpu.VMEM((2, half, d), bf),
                pltpu.VMEM((half, d), bf),
                pltpu.VMEM((2, half, d), bf),
                dma((14,)), dma((14,)), dma((16,)), dma((16,)),
                dma((14,)), dma((14,)), dma((16,)), dma((16,)),
                dma((2, ff // TILE)), dma((2,)), dma((2,)), dma((5,)), dma((4,)), dma((3,)), dma((2,)),
            ],
            compiler_params=pltpu.CompilerParams(
                collective_id=0, has_side_effects=True, vmem_limit_bytes=67043328
            ),
        )(x, w_gate, w_up, w_down)
        return result[0]

    return jax.shard_map(
        step,
        mesh=mesh,
        in_specs=(P(("dp", "tp"), None), P(None, "tp"), P(None, "tp"), P("tp", None)),
        out_specs=P(("dp", "tp"), None),
        check_vma=False,
    )
```

time: 511 us -> 411 us (0.80); the launches traced: 505 us -> 411 us
  Pallas kernels: 502 us -> 408 us
    pallas_call x1, Pallas kernels: 502 us -> 408 us  [step(): pl.pallas_call(_mlp_kernel, out_shape=[jax.ShapeDtypeStruct((n, d), bf),...]
where the time goes in v2:
time: 411 us
  Pallas kernels  408 us (99%)
    pallas_call x1, Pallas kernels, step(): pl.pallas_call(_mlp_kernel, out_shape=[jax.ShapeDtypeStruct((n, d), bf),...  408 us

profile of v2, /device:TPU:0, one launch (start us, length us, event | category | flops | bytes accessed | tf_op | source)
XLA Modules:
  0.0 410.9 jit_solution(1528980953522570505)
XLA Ops:
  0.0 407.7 %shard_map.46 = (bf16[224,5120]{1,0:T(8,128)(2,1)}, bf16[3584,5120]{1,0:T(8,128)(2,1)}, bf16[3584,2048]{1,0:T(8,128)(2,1)}, bf16[1792,5120]{1,0:T(8,128)(2,1)}, bf16[1568,5120]{1,0:T(8,128)(2,1)}) custom-call(bf16[224,5120]{1,0:T(8,128)(2,1)} %x.1, bf16[5120,2048]{1,0:T(8,128)(2,1)} %wg_hbm.1, bf16[5120,2048]{1,0:T(8,128)(2,1)} %wu_hbm.1, ...), custom_call_target="tpu_custom_call" | custom-call | tf_op jit(solution)/shard_map/pallas_call | solution.py:387
  407.7 3.2 copy.6

commit v3 on v2

--- a/solution.py
+++ b/solution.py
@@ -8,6 +8,8 @@
 MESH = pl.DeviceIdType.MESH
 TILE = 512
 EARLY = 256
+POLL_AT = 5
+SEND_AT = 3
 
 
 def _device(r, c):
@@ -100,7 +102,7 @@
     def fetch(src, dst, i):
         return pltpu.make_async_copy(src, dst, in_sem.at[i])
 
-    def add(q, to, sources):
+    def add(q, to, sources, first=0, last=dtiles):
         def tile(n, _):
             cols = span(n, 1, TILE)
             total = term[q % 2, :, cols] + pin[:, cols].astype(jnp.float32)
@@ -109,23 +111,27 @@
             to[:, cols] = total.astype(jnp.bfloat16)
             return 0
 
-        lax.fori_loop(0, dtiles, tile, 0)
+        lax.fori_loop(first, last, tile, 0)
 
     def early_copy(n):
         return pltpu.make_async_copy(
-            wd_hbm.at[:, span(n, 1, EARLY)], wd.at[n % 4], early_sem.at[n % 4]
+            wd_hbm.at[:, span(n, 1, EARLY)], wd.at[n % 5], early_sem.at[n % 5]
         )
 
     def early_terms():
         def tile(n, _):
             early_copy(n).wait()
 
-            @pl.when(n + 3 < d // EARLY)
-            def _():
-                early_copy(n + 3).start()
+            @pl.when(n == d // EARLY - 4)
+            def _():
+                ready(6)
+
+            @pl.when(n + 4 < d // EARLY)
+            def _():
+                early_copy(n + 4).start()
 
             cols = span(n, 1, EARLY)
-            prod = jnp.dot(hbuf[...], wd[n % 4], preferred_element_type=jnp.float32)
+            prod = jnp.dot(hbuf[...], wd[n % 5], preferred_element_type=jnp.float32)
             term[1, :, cols] = prod[:half]
             other[1, :, cols] = prod[half:n_rows].astype(jnp.bfloat16)
             term[0, :, cols] = prod[n_rows : n_rows + half]
@@ -150,51 +156,64 @@
         pl.semaphore_signal(barrier, inc=1, device_id={"tp": dev}, device_id_type=MESH)
     pl.semaphore_wait(barrier, 3)
 
+    for way in range(2):
+        dd_copy(0, way, own=True).start()
     for m in range(2):
         for way in range(2):
             ag_copy(m, way, own=True).start()
+    mine = [
+        pltpu.make_async_copy(
+            x.at[pl.ds((1 - way) * half, half)], xbuf.at[pl.ds(2 * way * half, half)], x_sem.at[way]
+        )
+        for way in range(2)
+    ]
+    theirs = [
+        pltpu.make_async_copy(
+            xg.at[rows(0, 1 - way, 1)], xbuf.at[pl.ds((2 * way + 1) * half, half)], h_sem.at[way]
+        )
+        for way in range(2)
+    ]
     for way in range(2):
-        dd_copy(0, way, own=True).start()
-    bounce = pltpu.make_async_copy(x, xbuf.at[pl.ds(n_rows, n_rows)], x_sem.at[0])
-    bounce.start()
+        mine[way].start()
     for n in range(ftiles):
         for k in range(2):
             w_copy(k, n).start()
-    bounce.wait()
-    stores = [
-        pltpu.make_async_copy(
-            xbuf.at[pl.ds((2 + h) * half, half)], xg.at[rows(0, h, 0)], x_sem.at[h]
-        )
-        for h in range(2)
-    ]
-    for s in stores:
-        s.start()
-    for s in stores:
-        s.wait()
     for way in range(2):
         dd_copy(0, way, own=True).wait_recv()
-    x_load(0, 0).start()
+        theirs[way].start()
+    for way in range(2):
+        mine[way].wait()
+        theirs[way].wait()
+
+    def poll(m):
+        for k in range(2):
+            ag_copy(m, k).wait_recv()
+            dd_copy(m + 1, k).start()
+
+            @pl.when(m < 5)
+            def _():
+                ag_copy(m + 2, k).start()
+
+    def ready(i):
+        for k in range(2):
+            dd_copy(i, k).wait_recv()
+        x_load(i, 0).start()
 
     def stage(i, _):
-        @pl.when(i == 6)
-        def _():
-            early_terms()
-
         def work(s, _):
             way, n = (s // 2) % 2, s // 4 * 2 + s % 2
 
             for k in range(2):
                 @pl.when(s == 2 * k)
                 def _():
-                    if k == 0:
-                        x_load(i, 1).start()
-                    x_load(i, k).wait()
-
                     @pl.when(i > 0)
                     def _():
+                        if k == 0:
+                            x_load(i, 1).start()
+                        x_load(i, k).wait()
                         h_store(i - 1, k).wait()
 
-            @pl.when((s == 4) & (i == 6))
+            @pl.when((s == SEND_AT) & (i == 6))
             def _():
                 early_send()
 
@@ -205,23 +224,20 @@
 
             @pl.when((s == 4) & (i == 5))
             def _():
-                for k in range(3):
+                for k in range(4):
                     early_copy(k).start()
 
             @pl.when((s == 6) & (i < 7))
             def _():
                 h_store(i, 0).start()
 
-            @pl.when((s == 7) & (i < 7))
-            def _():
-                for k in range(2):
-                    ag_copy(i, k).wait_recv()
-
-                    @pl.when(i < 5)
-                    def _():
-                        ag_copy(i + 2, k).start()
-
-                    dd_copy(i + 1, k).start()
+            @pl.when((s == POLL_AT) & (i < 7) & (i != 5))
+            def _():
+                poll(i)
+
+            @pl.when((s == 7) & (i < 7) & (i != 5))
+            def _():
+                ready(i + 1)
 
             for k in range(2):
                 @pl.when((i == 0) & (way == 0))
@@ -240,9 +256,11 @@
         @pl.when(i < 7)
         def _():
             h_store(i, 1).start()
-            for k in range(2):
-                dd_copy(i + 1, k).wait_recv()
-            x_load(i + 1, 0).start()
+
+        @pl.when(i == 5)
+        def _():
+            poll(5)
+            early_terms()
 
         return 0
 
@@ -269,18 +287,13 @@
         )
 
     def down(q):
-        @pl.when(q >= 4)
+        h_load(q).wait()
+
+        @pl.when(q >= 6)
         def _():
-            h_load(q).wait()
-
-        pt_copy(q - 2).wait_send()
+            pt_copy(q - 2).wait_send()
 
         def tile(n, _):
-            for k in range(5):
-                @pl.when((q == 2) & (n == 2 * k))
-                def _():
-                    wd_copy(k).wait()
-
             block = w[span(n // 2, 1, ff), span(n % 2, 1, TILE)]
             prod = jnp.dot(
                 hbuf[span(q % 2, 1, n_rows), :], block, preferred_element_type=jnp.float32
@@ -297,6 +310,61 @@
         def _():
             h_load(q + 2).start()
 
+    def far_terms():
+        cut = d // 2
+
+        def part(i):
+            return pl.ds(i * cut, cut)
+
+        def pt_part(q, i):
+            return remote(
+                other.at[q % 2, :, part(i)], slot(parts, q).at[:, part(i)],
+                pt_send, pt_recv, q + 14 * i, partner,
+            )
+
+        def tile(n, _):
+            for k in range(5):
+                @pl.when(n == 2 * k)
+                def _():
+                    wd_copy(k).wait()
+
+            block = w[span(n // 2, 1, ff), span(n % 2, 1, TILE)]
+            prod = jnp.dot(hbuf[...], block, preferred_element_type=jnp.float32)
+            cols = span(n, 1, TILE)
+            for k in range(2):
+                term[k, :, cols] = prod[2 * k * half : (2 * k + 1) * half]
+                other[k, :, cols] = prod[(2 * k + 1) * half : 2 * (k + 1) * half].astype(jnp.bfloat16)
+            return 0
+
+        def pass_on(i):
+            for q in (2, 3):
+                pt_part(q, i).wait_recv()
+                own = fetch(slot(parts, q).at[:, part(i)], pin.at[:, part(i)], 0)
+                own.start()
+                own.wait()
+                to = slot(xbuf, (q - 2) * 2 + 1)
+                add(q, to, 0, i * dtiles // 2, (i + 1) * dtiles // 2)
+                remote(
+                    to.at[:, part(i)], slot(sums, (q - 2) * 7 + 1).at[:, part(i)],
+                    rs_send, rs_recv, (q - 2) * 7 + 1, ring[q - 2],
+                ).start()
+
+        for q in range(2):
+            pt_copy(q).wait_send()
+        lax.fori_loop(0, dtiles // 2, tile, 0)
+        for q in (2, 3):
+            pt_part(q, 0).start()
+        lax.fori_loop(dtiles // 2, dtiles - 2, tile, 0)
+        pass_on(0)
+        lax.fori_loop(dtiles - 2, dtiles, tile, 0)
+        for q in (2, 3):
+            pt_part(q, 1).start()
+            h_load(q + 2).start()
+        pass_on(1)
+        for i in range(2):
+            for q in (2, 3):
+                pt_part(q, i).wait_send()
+
     def send(q, way):
         m = q // 2
         pt_copy(q).wait_recv()
@@ -304,25 +372,13 @@
         own.start()
         before = m - 2 + m // 6
 
-        @pl.when(m >= 2)
-        def _():
-            rs_copy(before, way).wait_recv()
-            rs_copy(m - 2, way).wait_send()
-            got = fetch(slot(sums, way * 7 + before), rin.at[0], 1)
-            got.start()
-            got.wait()
-
+        rs_copy(before, way).wait_recv()
+        rs_copy(m - 2, way).wait_send()
+        got = fetch(slot(sums, way * 7 + before), rin.at[0], 1)
+        got.start()
+        got.wait()
         own.wait()
-        to = slot(xbuf, way * 2 + m % 2)
-
-        @pl.when(m >= 2)
-        def _():
-            add(q, to, 1)
-
-        @pl.when(m < 2)
-        def _():
-            add(q, to, 0)
-
+        add(q, slot(xbuf, way * 2 + m % 2), 1)
         rs_copy(m, way).start()
 
     def finish(q):
@@ -344,12 +400,13 @@
     def step(q, _):
         down(q)
         for way in range(2):
-            @pl.when((q > 2) & ((q - 1) % 2 == way))
+            @pl.when((q > 4) & ((q - 1) % 2 == way))
             def _():
                 send(q - 1, way)
         return 0
 
-    lax.fori_loop(2, 15, step, 0)
+    far_terms()
+    lax.fori_loop(4, 15, step, 0)
     down(15)
 
     def drain(m, _):
@@ -398,15 +455,15 @@
             scratch_shapes=[
                 pltpu.VMEM((2 * d, ff), bf),
                 pltpu.VMEM((4 * half, d), bf),
-                pltpu.VMEM((4, ff, EARLY), bf),
+                pltpu.VMEM((5, ff, EARLY), bf),
                 pltpu.VMEM((2 * n, ff), bf),
                 pltpu.VMEM((2, half, d), jnp.float32),
                 pltpu.VMEM((2, half, d), bf),
                 pltpu.VMEM((half, d), bf),
                 pltpu.VMEM((2, half, d), bf),
                 dma((14,)), dma((14,)), dma((16,)), dma((16,)),
-                dma((14,)), dma((14,)), dma((16,)), dma((16,)),
-                dma((2, ff // TILE)), dma((2,)), dma((2,)), dma((5,)), dma((4,)), dma((3,)), dma((2,)),
+                dma((14,)), dma((14,)), dma((18,)), dma((18,)),
+                dma((2, ff // TILE)), dma((2,)), dma((2,)), dma((5,)), dma((5,)), dma((3,)), dma((2,)),
             ],
             compiler_params=pltpu.CompilerParams(
                 collective_id=0, has_side_effects=True, vmem_limit_bytes=67043328

time: 411 us -> 399 us (0.971)
  Pallas kernels: 408 us -> 395 us
    pallas_call x1, Pallas kernels: 408 us -> 395 us  [step(): pl.pallas_call(_mlp_kernel, out_shape=[jax.ShapeDtypeStruct((n, d), bf),...]
where the time goes in v3:
time: 399 us; the launch traced here: 398 us
  Pallas kernels  395 us (99%)
    pallas_call x1, Pallas kernels, step(): pl.pallas_call(_mlp_kernel, out_shape=[jax.ShapeDtypeStruct((n, d), bf),...  395 us

profile of v3, /device:TPU:0, one launch (start us, length us, event | category | flops | bytes accessed | tf_op | source)
XLA Modules:
  0.0 398.2 jit_solution(13380759588101502884)
XLA Ops:
  0.0 395.0 %shard_map.46 = (bf16[224,5120]{1,0:T(8,128)(2,1)}, bf16[3584,5120]{1,0:T(8,128)(2,1)}, bf16[3584,2048]{1,0:T(8,128)(2,1)}, bf16[1792,5120]{1,0:T(8,128)(2,1)}, bf16[1568,5120]{1,0:T(8,128)(2,1)}) custom-call(bf16[224,5120]{1,0:T(8,128)(2,1)} %x.1, bf16[5120,2048]{1,0:T(8,128)(2,1)} %wg_hbm.1, bf16[5120,2048]{1,0:T(8,128)(2,1)} %wu_hbm.1, ...), custom_call_target="tpu_custom_call" | custom-call | tf_op jit(solution)/shard_map/pallas_call | solution.py:444
  395.0 3.2 copy.6

commit v4 on v3

--- a/solution.py
+++ b/solution.py
@@ -381,33 +381,70 @@
         add(q, slot(xbuf, way * 2 + m % 2), 1)
         rs_copy(m, way).start()
 
-    def finish(q):
-        way = q - 14
-        h = 1 - way
+    def fold(q, kept):
+        way = q % 2
         pt_copy(q).wait_recv()
-        own = fetch(slot(parts, q), pin, 0)
-        own.start()
-        last = ((4, 6), (6, 4))[way]
-        for k in range(2):
-            rs_copy(last[k], k).wait_recv()
-            fetch(slot(sums, k * 7 + last[k]), rin.at[k], 1 + k).start()
-        for k in range(2):
-            fetch(slot(sums, k * 7 + last[k]), rin.at[k], 1 + k).wait()
-        own.wait()
-        add(q, other.at[way], 2)
-        pltpu.make_async_copy(other.at[way], out.at[pl.ds(h * half, half)], y_sem.at[way]).start()
-
-    def step(q, _):
-        down(q)
-        for way in range(2):
-            @pl.when((q > 4) & ((q - 1) % 2 == way))
-            def _():
-                send(q - 1, way)
+        loads = [fetch(slot(parts, q), pin, 0)]
+        if kept is not None:
+            rs_copy(kept, way).wait_recv()
+            loads.append(fetch(slot(sums, way * 7 + kept), rin.at[0], 1))
+        for load in loads:
+            load.start()
+        for load in loads:
+            load.wait()
+
+        def tile(n, _):
+            cols = span(n, 1, TILE)
+            total = term[q % 2, :, cols] + pin[:, cols].astype(jnp.float32)
+            if kept is not None:
+                total += rin[0, :, cols].astype(jnp.float32)
+            term[q % 2, :, cols] = total
+            return 0
+
+        lax.fori_loop(0, dtiles, tile, 0)
+
+    def last_add(k, src, to, i):
+        def tile(n, _):
+            cols = span(n, 1, TILE)
+            to[:, cols] = (term[k, :, cols] + rin[src, :, cols].astype(jnp.float32)).astype(jnp.bfloat16)
+            return 0
+
+        lax.fori_loop(i * dtiles // 2, (i + 1) * dtiles // 2, tile, 0)
+
+    def arrive(m):
+        for way in range(2):
+            rs_copy(m, way).wait_recv()
+            fetch(slot(sums, way * 7 + m), rin.at[way], 1 + way).start()
+        for way in range(2):
+            fetch(slot(sums, way * 7 + m), rin.at[way], 1 + way).wait()
+
+    def columns(i):
+        return pl.ds(i * (d // 2), d // 2)
+
+    def message(m, _):
+        for way in range(2):
+            down(2 * m + way)
+        for way in range(2):
+            send(2 * m + way, way)
         return 0
 
     far_terms()
-    lax.fori_loop(4, 15, step, 0)
-    down(15)
+    lax.fori_loop(2, 6, message, 0)
+
+    for way in range(2):
+        down(12 + way)
+    for way in range(2):
+        fold(12 + way, None)
+        rs_copy(4, way).wait_send()
+    arrive(5)
+    for i in range(2):
+        for way in range(2):
+            to = slot(xbuf, way * 2)
+            last_add(way, way, to, i)
+            remote(
+                to.at[:, columns(i)], slot(sums, way * 7 + 6).at[:, columns(i)],
+                rs_send, rs_recv, way * 7 + 6, ring[way],
+            ).start()
 
     def drain(m, _):
         for way in range(2):
@@ -419,18 +456,30 @@
             dd_copy(i, way).wait_send()
         return 0
 
+    for way in range(2):
+        down(14 + way)
     lax.fori_loop(0, 7, drain, 0)
     lax.fori_loop(0, 8, drain_pair, 0)
-    pt_copy(14).wait_send()
-    finish(14)
-    pt_copy(15).wait_send()
-    finish(15)
-    for way in range(2):
-        pltpu.make_async_copy(
-            other.at[way], out.at[pl.ds((1 - way) * half, half)], y_sem.at[way]
-        ).wait()
-        for m in (5, 6):
-            rs_copy(m, way).wait_send()
+    for way in range(2):
+        fold(14 + way, 4)
+        pt_copy(14 + way).wait_send()
+        rs_copy(5, way).wait_send()
+    arrive(6)
+
+    def result(k, i):
+        return pltpu.make_async_copy(
+            other.at[k, :, columns(i)], out.at[pl.ds((1 - k) * half, half), columns(i)], y_sem.at[k, i]
+        )
+
+    for i in range(2):
+        for k in range(2):
+            last_add(k, 1 - k, other.at[k], i)
+            result(k, i).start()
+    for i in range(2):
+        for k in range(2):
+            result(k, i).wait()
+    for way in range(2):
+        rs_copy(6, way).wait_send()
 
 
 def solution(mesh):
@@ -463,7 +512,7 @@
                 pltpu.VMEM((2, half, d), bf),
                 dma((14,)), dma((14,)), dma((16,)), dma((16,)),
                 dma((14,)), dma((14,)), dma((18,)), dma((18,)),
-                dma((2, ff // TILE)), dma((2,)), dma((2,)), dma((5,)), dma((5,)), dma((3,)), dma((2,)),
+                dma((2, ff // TILE)), dma((2,)), dma((2,)), dma((5,)), dma((5,)), dma((3,)), dma((2, 2)),
             ],
             compiler_params=pltpu.CompilerParams(
                 collective_id=0, has_side_effects=True, vmem_limit_bytes=67043328

time: 399 us -> 389 us (0.975)
  Pallas kernels: 395 us -> 385 us
    pallas_call x1, Pallas kernels: 395 us -> 385 us  [step(): pl.pallas_call(_mlp_kernel, out_shape=[jax.ShapeDtypeStruct((n, d), bf),...]
where the time goes in v4:
time: 389 us; the launch traced here: 388 us
  Pallas kernels  385 us (99%)
    pallas_call x1, Pallas kernels, step(): pl.pallas_call(_mlp_kernel, out_shape=[jax.ShapeDtypeStruct((n, d), bf),...  385 us

profile of v4, /device:TPU:0, one launch (start us, length us, event | category | flops | bytes accessed | tf_op | source)
XLA Modules:
  0.0 388.2 jit_solution(7008013726388395258)
XLA Ops:
  0.0 385.0 %shard_map.46 = (bf16[224,5120]{1,0:T(8,128)(2,1)}, bf16[3584,5120]{1,0:T(8,128)(2,1)}, bf16[3584,2048]{1,0:T(8,128)(2,1)}, bf16[1792,5120]{1,0:T(8,128)(2,1)}, bf16[1568,5120]{1,0:T(8,128)(2,1)}) custom-call(bf16[224,5120]{1,0:T(8,128)(2,1)} %x.1, bf16[5120,2048]{1,0:T(8,128)(2,1)} %wg_hbm.1, bf16[5120,2048]{1,0:T(8,128)(2,1)} %wu_hbm.1, ...), custom_call_target="tpu_custom_call" | custom-call | tf_op jit(solution)/shard_map/pallas_call | solution.py:493
  385.0 3.2 copy.6
